TPU v7x, 32 devices: a whole 2x2x4 slice. The times are simulated.
32 devices in a mesh: dp: 4 (over y, x), vocab: 8 (over z, core).
Axes of the slice: x: 2, y: 2, z: 4, core: 2. Of those that a mesh axis runs over, the one named last changes fastest.
Arguments:
- logits: bfloat16 [32, 8, 152064], P('dp', None, 'vocab'), may hold values from -40 to 250
- draft_probs: bfloat16 [32, 8, 152064], P('dp', None, 'vocab'), may hold values from 5.9185606e-07 to 1, as said below
- draft_tokens: int32 [32, 8], P('dp'), may hold values from 0 to 152063
- draft_lengths: int32 [32], P('dp'), may hold values from 1 to 8
- owner_group: int32 [32], P('dp'), may hold values from 0 to 3, as said below
Outputs:
- correction: bfloat16 [64, 152064], P('dp', 'vocab')
- accept_ratio: float32 [64, 8], P('dp')
- expected_accepted: float32 [64], P('dp')
Inputs may be any that keep to these rules, and one draw needn't show every extreme that they name: Each row of draft_probs is a distribution over the whole vocabulary whose entries are all positive. `owner_group`: no group hands more than 4 sequences to one group; some group receives exactly 4 sequences from every group.
All inputs are finite; a program needn't handle non-finite values.
Results may differ from a plain program's by a relative error of at most 0.001.
Values may be sent and summed in bfloat16 or wider, within the bound.
A program may use at most 64 MiB of HBM per device.

v0:
```python
import jax
import jax.numpy as jnp
from jax import lax
from jax.sharding import PartitionSpec as P

mixing = 0.1


def verify(logits, draft_probs, tokens, lengths):
    scores = logits.astype(jnp.float32)
    shard_width = scores.shape[2]
    column = (
        lax.broadcasted_iota(jnp.int32, scores.shape, 2) + lax.axis_index("vocab") * shard_width
    )
    is_drafted = column == tokens[:, :, None]
    proposal = draft_probs.astype(jnp.float32)
    drafted_local = jnp.sum(jnp.where(is_drafted, proposal, 0.0), axis=2)
    top = lax.pmax(jnp.max(scores, axis=2), "vocab")
    shifted = jnp.exp(scores - top[:, :, None])
    row_total, chosen, drafted = lax.psum(
        (
            jnp.sum(shifted, axis=2),
            jnp.sum(jnp.where(is_drafted, shifted, 0.0), axis=2),
            drafted_local,
        ),
        "vocab",
    )
    target = shifted / row_total[:, :, None]
    excess = jnp.maximum(target - proposal, 0.0)
    spread = lax.psum(jnp.sum(excess, axis=2), "vocab")
    residual = (excess + mixing * target) / (spread + mixing)[:, :, None]
    position = lax.broadcasted_iota(jnp.int32, tokens.shape, 1)
    is_live = position < lengths[:, None]
    safe_draft = jnp.where(is_live, drafted, 1.0)
    accept = jnp.where(is_live, jnp.minimum(1.0, chosen / row_total / safe_draft), 0.0)
    survive = jnp.cumprod(accept, axis=1)
    before = jnp.concatenate([jnp.ones_like(survive[:, :1]), survive[:, :-1]], axis=1)
    weight = jnp.where(is_live, before * (1.0 - accept), 0.0)
    corrected = jnp.sum(weight[:, :, None] * residual, axis=1).astype(jnp.bfloat16)
    expected = jnp.sum(survive, axis=1)
    return (corrected, accept, expected)


def routing(owners, capacity, groups):
    seq_count = owners.shape[0]
    earlier = lax.broadcasted_iota(jnp.int32, (seq_count, seq_count), 1) < lax.broadcasted_iota(
        jnp.int32, (seq_count, seq_count), 0
    )
    same = owners[:, None] == owners[None, :]
    slot_rank = jnp.sum(jnp.where(same & earlier, 1, 0), axis=1)
    target_slot = owners * capacity + slot_rank
    slot_rows = lax.broadcasted_iota(jnp.int32, (groups * capacity, seq_count), 0)
    return slot_rows == target_slot[None, :]


def body(logits, draft_probs, draft_tokens, draft_lengths, owner_group):
    groups = lax.axis_size("dp")
    seq_count = owner_group.shape[0]
    capacity = max(2, 2 * seq_count // groups)
    select = routing(owner_group, capacity, groups)
    picker = select.astype(jnp.bfloat16)
    corrected, accept, expected = verify(logits, draft_probs, draft_tokens, draft_lengths)
    outgoing = jnp.dot(picker, corrected, preferred_element_type=jnp.float32).astype(jnp.bfloat16)
    correction = lax.all_to_all(outgoing, "dp", split_axis=0, concat_axis=0, tiled=True)
    sent_accept = jnp.sum(jnp.where(select[:, :, None], accept[None, :, :], 0.0), axis=1)
    sent_expected = jnp.sum(jnp.where(select, expected[None, :], 0.0), axis=1)
    accept_ratio, expected_accepted = (
        lax.all_to_all(sent_accept, "dp", split_axis=0, concat_axis=0, tiled=True),
        lax.all_to_all(sent_expected, "dp", split_axis=0, concat_axis=0, tiled=True),
    )
    return (correction, accept_ratio, expected_accepted)


def solution(mesh):
    placed = (P("dp", None, "vocab"), P("dp", None, "vocab"), P("dp", None), P("dp"), P("dp"))
    return jax.shard_map(
        body,
        mesh=mesh,
        in_specs=placed,
        out_specs=(P("dp", "vocab"), P("dp", None), P("dp")),
        check_vma=False,
    )
```

profile of v0, /device:TPU:0, one launch (start us, length us, event | category | flops | bytes accessed | tf_op | source)
XLA Modules:
  0.0 98.8 jit_solution(12494934219520476122)
XLA Ops:
  0.6 0.0 copy-start
  0.6 0.0 copy-start.1
  0.7 1.0 %select_reduce_fusion.2 = s32[8]{0:T(128)S(1)} fusion(s32[8]{0:T(128)} %param.9), kind=kLoop, calls=%fused_computation.19 | loop fusion | flops 312 | bytes 64 | tf_op jit(solution)/shard_map/reduce_sum | solution.py:50
  1.7 0.7 multiply_add_fusion
  2.3 2.2 %reduce_max.14 = bf16[8,8]{1,0:T(8,128)(2,1)S(1)} reduce(bf16[8,8,19008]{2,1,0:T(8,128)(2,1)} %param.5, bf16[]{:T(256)} %constant.14.clone.1), dimensions={2}, to_apply=%region_1.2 | reduce | flops 1216448 | bytes 2433154 | tf_op jit(solution)/shard_map/reduce_max | solution.py:18
  4.5 18.1 %pmax.7 = f32[8,8]{1,0:T(8,128)S(1)} all-reduce(bf16[8,8]{1,0:T(8,128)(2,1)S(1)} %reduce_max.14), channel_id=1, replica_groups=mesh['dp'=4,'vocab'=8] {'vocab'}, use_global_device_ids=true, to_apply=%region_2.3 | all-reduce | flops 64 | bytes 384 | tf_op jit(solution)/shard_map/pmax | solution.py:18
  22.6 0.0 copy-done
  22.6 0.0 copy-done.1
  22.6 1.7 %fusion.1 = (f32[8,8]{1,0:T(8,128)S(1)}, f32[8,8]{1,0:T(8,128)S(1)}) fusion(bf16[8,8,19008]{2,1,0:T(8,128)(2,1)S(1)} %copy-done, f32[8,8]{1,0:T(8,128)S(1)} %pmax.7, s32[8,8]{1,0:T(8,128)S(1)} %copy-done.1, s32[19008]{0:T(1024)S(1)} %iota_add_fusion), kind=kLoop, calls=%fused_computation.5 | loop fusion | flops 7298944 | bytes 2510080 | tf_op jit(solution)/shard_map/reduce_sum | solution.py:23
  24.3 13.6 %psum.29 = f32[8,8]{1,0:T(8,128)S(1)} all-reduce(f32[8,8]{1,0:T(8,128)S(1)} %get-tuple-element.13), channel_id=1, replica_groups=mesh['dp'=4,'vocab'=8] {'vocab'}, use_global_device_ids=true, to_apply=%region_6.7 | all-reduce | flops 64 | bytes 512 | tf_op jit(solution)/shard_map/psum | solution.py:20
  37.9 0.0 copy-start.2
  37.9 3.9 %fusion.2 = (f32[8,8]{1,0:T(8,128)S(1)}, f32[8,8]{1,0:T(8,128)S(1)}) fusion(bf16[8,8,19008]{2,1,0:T(8,128)(2,1)} %param.6, s32[8,8]{1,0:T(8,128)S(1)} %copy-done.1, s32[19008]{0:T(1024)S(1)} %iota_add_fusion, f32[8,8]{1,0:T(8,128)S(1)} %psum.29, f32[8,8]{1,0:T(8,128)S(1)} %pmax.7, bf16[8,8,19008]{2,1,0:T(8,128)(2,1)S(1)} %copy-done), kind=kLoop, calls=%fused_computation.6 | loop fusion | flops 12164992 | bytes 4943360 | tf_op jit(solution)/shard_map/reduce_sum | solution.py:17
  41.8 25.9 %all-reduce.1 = (f32[8,8]{1,0:T(8,128)S(1)}, f32[8,8]{1,0:T(8,128)S(1)}, f32[8,8]{1,0:T(8,128)S(1)}) all-reduce(f32[8,8]{1,0:T(8,128)S(1)} %get-tuple-element.15, f32[8,8]{1,0:T(8,128)S(1)} %get-tuple-element.12, f32[8,8]{1,0:T(8,128)S(1)} %get-tuple-element.14), channel_id=1, replica_groups=mesh['dp'=4,'vocab'=8] {'vocab'}, use_global_device_ids=true, to_apply=%region_11.12 | all-reduce | flops 192 | bytes 1536 | tf_op jit(solution)/shard_map/psum | solution.py:30
  67.7 0.0 copy-done.2
  67.7 0.1 minimum_select_fusion
  67.8 0.2 reduce_window.9
  68.0 0.1 reduce_sum.88
  68.1 0.1 select_reduce_fusion.1
  68.2 0.7 all_to_all.30
  68.8 3.7 %all-to-all-start.2 = ((f32[4,4,1]{1,2,0:T(1,128)}), f32[4,4,1]{1,2,0:T(1,128)S(1)}, u32[]{:S(2)}, u32[]{:S(2)}) async-start(f32[4,4,1]{1,2,0:T(1,128)} %bitcast.2), calls=%async_computation.2 | async-start | bytes 4096 | tf_op jit(solution)/shard_map/all_to_all | solution.py:69
  72.6 0.1 iota_compare_fusion.2
  72.6 0.1 select_reduce_fusion
  72.7 0.1 multiply_select_fusion
  72.8 0.7 copy.11
  73.5 4.8 %multiply_reduce_fusion = bf16[8,19008]{1,0:T(8,128)(2,1)S(1)} fusion(bf16[8,8,19008]{2,1,0:T(8,128)(2,1)} %param.6, bf16[8,8,19008]{2,1,0:T(8,128)(2,1)S(1)} %copy-done, f32[8,8]{1,0:T(8,128)S(1)} %get-tuple-element.20, f32[8,8]{1,0:T(8,128)S(1)} %psum.29, f32[8,8]{1,0:T(8,128)S(1)} %multiply_select_fusion, f32[8,8]{1,0:T(8,128)S(1)} %pmax.7), kind=kLoop, calls=%fused_computation.7 | loop fusion | flops 13229568 | bytes 5171200 | tf_op jit(solution)/shard_map/reduce_sum | solution.py:39
  78.3 0.0 all-to-all-done.2
  78.3 4.2 %all-to-all-start.1 = ((f32[4,4,8]{2,1,0:T(4,128)}), f32[4,4,8]{2,1,0:T(4,128)S(1)}, u32[]{:S(2)}, u32[]{:S(2)}) async-start(f32[4,4,8]{2,1,0:T(4,128)} %bitcast), calls=%async_computation.1 | async-start | bytes 16384 | tf_op jit(solution)/shard_map/all_to_all | solution.py:68
  82.5 0.4 convolution_convert_fusion
  82.9 1.0 all_to_all.24
  83.9 3.3 %all-to-all-done.1 = f32[4,4,8]{2,1,0:T(4,128)S(1)} async-done(((f32[4,4,8]{2,1,0:T(4,128)}), f32[4,4,8]{2,1,0:T(4,128)S(1)}, u32[]{:S(2)}, u32[]{:S(2)}) %all-to-all-start.1) | async-done | bytes 544 | tf_op jit(solution)/shard_map/all_to_all | solution.py:68
  87.2 3.5 %all-to-all-start = ((bf16[4,4,19008]{2,1,0:T(4,128)(2,1)}), bf16[4,4,19008]{2,1,0:T(4,128)(2,1)S(1)}, u32[]{:S(2)}, u32[]{:S(2)}) async-start(bf16[4,4,19008]{2,1,0:T(4,128)(2,1)} %all_to_all.24), calls=%async_computation | async-start | bytes 1220608 | tf_op jit(solution)/shard_map/all_to_all | solution.py:64
  90.6 0.5 broadcast.32
  91.2 0.7 reduce.4
  91.8 0.6 all_to_all.32
  92.4 0.7 copy.13
  93.1 4.6 %all-to-all-done = bf16[4,4,19008]{2,1,0:T(4,128)(2,1)S(1)} async-done(((bf16[4,4,19008]{2,1,0:T(4,128)(2,1)}), bf16[4,4,19008]{2,1,0:T(4,128)(2,1)S(1)}, u32[]{:S(2)}, u32[]{:S(2)}) %all-to-all-start) | async-done | bytes 608288 | tf_op jit(solution)/shard_map/all_to_all | solution.py:64
  97.7 1.1 %all_to_all.26 = bf16[16,19008]{1,0:T(8,128)(2,1)} reshape(bf16[4,4,19008]{2,1,0:T(4,128)(2,1)S(1)} %all-to-all-done) | data formatting | bytes 1216512 | tf_op jit(solution)/shard_map/all_to_all | solution.py:64
  (1 shorter events, 0.0 us)
Async XLA Ops:
  0.6 22.0 %copy-start = (bf16[8,8,19008]{2,1,0:T(8,128)(2,1)S(1)}, bf16[8,8,19008]{2,1,0:T(8,128)(2,1)}, u32[]{:S(2)}) copy-start(bf16[8,8,19008]{2,1,0:T(8,128)(2,1)} %param.5) | copy-start | bytes 7299076
  0.6 22.0 %copy-start.1 = (s32[8,8]{1,0:T(8,128)S(1)}, s32[8,8]{1,0:T(8,128)}, u32[]{:S(2)}) copy-start(s32[8,8]{1,0:T(8,128)} %param.7) | copy-start | bytes 772
  37.9 29.8 %copy-start.2 = (s32[8]{0:T(128)S(1)}, s32[8]{0:T(128)}, u32[]{:S(2)}) copy-start(s32[8]{0:T(128)} %param.8) | copy-start | bytes 100
  68.8 9.4 %all-to-all-start.2 = ((f32[4,4,1]{1,2,0:T(1,128)}), f32[4,4,1]{1,2,0:T(1,128)S(1)}, u32[]{:S(2)}, u32[]{:S(2)}) async-start(f32[4,4,1]{1,2,0:T(1,128)} %bitcast.2), calls=%async_computation.2 | async-start | bytes 4096 | tf_op jit(solution)/shard_map/all_to_all | solution.py:69
  78.3 8.9 %all-to-all-start.1 = ((f32[4,4,8]{2,1,0:T(4,128)}), f32[4,4,8]{2,1,0:T(4,128)S(1)}, u32[]{:S(2)}, u32[]{:S(2)}) async-start(f32[4,4,8]{2,1,0:T(4,128)} %bitcast), calls=%async_computation.1 | async-start | bytes 16384 | tf_op jit(solution)/shard_map/all_to_all | solution.py:68
  87.2 10.5 %all-to-all-start = ((bf16[4,4,19008]{2,1,0:T(4,128)(2,1)}), bf16[4,4,19008]{2,1,0:T(4,128)(2,1)S(1)}, u32[]{:S(2)}, u32[]{:S(2)}) async-start(bf16[4,4,19008]{2,1,0:T(4,128)(2,1)} %all_to_all.24), calls=%async_computation | async-start | bytes 1220608 | tf_op jit(solution)/shard_map/all_to_all | solution.py:64
where the time goes:
time: 99.2 us; the launch traced here: 98.8 us
  blocking collectives  57.6 us (58%)
  other arithmetic  15.6 us (16%)
  starting transfers between devices  11.4 us (11%)
  waiting for transfers between devices  7.9 us (8%)
  local copies, waits for them, and re-layouts  5.16 us (5%)
    psum x1, blocking collectives, verify(): spread = lax.psum(jnp.sum(excess, axis=2), 'vocab')  25.9 us
    pmax x1, blocking collectives, verify(): top = lax.pmax(jnp.max(scores, axis=2), 'vocab')  18.1 us
    psum x1, blocking collectives, verify(): lax.psum((jnp.sum(shifted, axis=2), jnp.sum(jnp.where(is_drafted, shifted...  13.6 us
    reduce_sum x1, other arithmetic, verify(): jnp.sum(weight[:, :, None] * residual, axis=1).astype(jnp.bfloat16)  4.79 us
    all_to_all x1, waiting for transfers between devices, body(): lax.all_to_all(outgoing, 'dp', split_axis=0, concat_axis=0, tiled=True)  4.61 us
    all_to_all x1, starting transfers between devices, body(): lax.all_to_all(sent_accept, 'dp', split_axis=0, concat_axis=0, tiled=True)  4.2 us
    reduce_sum x1, other arithmetic, verify(): drafted_local = jnp.sum(jnp.where(is_drafted, proposal, 0.0), axis=2)  3.89 us
    all_to_all x1, starting transfers between devices, body(): lax.all_to_all(sent_expected, 'dp', split_axis=0, concat_axis=0, tiled=True)  3.72 us
  transfers between devices with their start and end apart: 3, of which 2 were waited for; matrix products, arithmetic and copies ran while one was open for 8% of the time, Pallas kernels for 0%

commit v1 on v0

v1 whole, which is shorter than its diff:
```python
import functools

import jax
import jax.numpy as jnp
from jax import lax
from jax.experimental import pallas as pl
from jax.experimental.pallas import tpu as pltpu
from jax.sharding import PartitionSpec as P

mixing = 0.1
LANES = 128
GROUP = 8
CHUNKS = 4
LOW = -1e30
MESH = pl.DeviceIdType.MESH


def sweep(start, stop, fn, carry):
    whole = (stop - start) // GROUP

    def step(i, c):
        base = start + i * GROUP
        return fn(base, GROUP, c)

    if whole:
        carry = lax.fori_loop(0, whole, step, carry)
    rest = (stop - start) % GROUP
    if rest:
        carry = fn(start + whole * GROUP, rest, carry)
    return carry


def lane_tile(i):
    return pl.ds(pl.multiple_of(i * LANES, LANES), LANES)


def kernel(
    dims,
    tok, lens, own, x_hbm, d_hbm,
    out, small_out,
    x, d, e, send, stat_in, spread_in, small,
    load_sem, stat_ssem, stat_rsem, spr_ssem, spr_rsem, out_ssem, out_rsem, sm_ssem, sm_rsem, local_sem,
):
    groups, vocab, capacity = dims
    seqs, depth, width = x_hbm.shape
    full = width // LANES
    tail = width - full * LANES
    tiles = e.shape[0]
    my_dp = lax.axis_index("dp")
    my_v = lax.axis_index("vocab")

    loads = []
    for n in range(seqs):
        loads.append(pltpu.make_async_copy(x_hbm.at[n], x.at[n], load_sem.at[n]))
    for n in range(seqs):
        loads.append(pltpu.make_async_copy(d_hbm.at[n], d.at[n], load_sem.at[seqs + n]))
    for n in range(seqs):
        loads[n].start()
        loads[seqs + n].start()

    barrier = pltpu.get_barrier_semaphore()
    v_peers = [lax.rem(my_v + k, vocab) for k in range(1, vocab)]
    g_peers = [lax.rem(my_dp + k, groups) for k in range(1, groups)]
    for p in v_peers:
        pl.semaphore_signal(barrier, inc=1, device_id=(my_dp, p), device_id_type=MESH)
    for p in g_peers:
        pl.semaphore_signal(barrier, inc=1, device_id=(p, my_v), device_id_type=MESH)

    sub = lax.broadcasted_iota(jnp.int32, (depth, LANES), 0)
    lane = lax.broadcasted_iota(jnp.int32, (depth, LANES), 1)
    zero = jnp.zeros((depth, LANES), jnp.float32)

    def tail_tile(ref, n, fill):
        part = ref[n, :, pl.ds(full * LANES, tail)].astype(jnp.float32)
        return jnp.concatenate([part, jnp.full((depth, LANES - tail), fill, jnp.float32)], axis=1)

    tops = zero
    sums = zero
    column0 = my_v * width
    for n in range(seqs):
        loads[n].wait()
        spot = jnp.zeros((depth, LANES), jnp.int32)
        for j in range(depth):
            spot = jnp.where(sub == j, tok[n, j], spot)
        spot = spot - column0 - lane

        def peak(base, count, c, n=n):
            c = list(c)
            for k in range(count):
                c[k % 4] = jnp.maximum(c[k % 4], x[n, :, lane_tile(base + k)].astype(jnp.float32))
            return tuple(c)

        first = tail_tile(x, n, LOW) if tail else jnp.full((depth, LANES), LOW, jnp.float32)
        c = sweep(0, full, peak, (first,) * 4)
        top = jnp.maximum(jnp.maximum(c[0], c[1]), jnp.maximum(c[2], c[3]))
        top = jnp.broadcast_to(jnp.max(top, axis=1, keepdims=True), (depth, LANES))

        loads[seqs + n].wait()

        def expo(base, count, c, n=n, top=top, spot=spot):
            c = list(c)
            for k in range(count):
                raw = x[n, :, lane_tile(base + k)].astype(jnp.float32)
                value = jnp.exp(raw - top)
                e[base + k, pl.ds(n * depth, depth), :] = value
                c[k % 4] = c[k % 4] + value
                hit = spot == (base + k) * LANES
                c[4] = jnp.where(hit, raw, c[4])
                c[5] = jnp.where(hit, d[n, :, lane_tile(base + k)].astype(jnp.float32), c[5])
            return tuple(c)

        first = zero
        picked_x = zero
        picked_d = zero
        if tail:
            raw = tail_tile(x, n, LOW)
            first = jnp.exp(raw - top)
            e[full, pl.ds(n * depth, depth), :] = first
            hit = (spot == full * LANES) & (lane < tail)
            picked_x = jnp.where(hit, raw, zero)
            picked_d = jnp.where(hit, tail_tile(d, n, 0.0), zero)
        c = sweep(0, full, expo, (first, zero, zero, zero, picked_x, picked_d))
        total = jnp.sum((c[0] + c[1]) + (c[2] + c[3]), axis=1, keepdims=True)
        tops = jnp.where(lax.rem(lane, seqs) == n, top, tops)
        sums = jnp.where(lane == n, total, sums)
        sums = jnp.where(lane == seqs + n, jnp.sum(c[4], axis=1, keepdims=True), sums)
        sums = jnp.where(lane == 2 * seqs + n, jnp.sum(c[5], axis=1, keepdims=True), sums)

    pl.semaphore_wait(barrier, vocab - 1 + groups - 1)

    def exchange(buf, ssem, rsem):
        copies = []
        for k in range(1, vocab):
            to = lax.rem(my_v + k, vocab)
            copies.append(pltpu.make_async_remote_copy(
                src_ref=buf.at[my_v], dst_ref=buf.at[my_v],
                send_sem=ssem.at[k], recv_sem=rsem.at[my_v],
                device_id=(my_dp, to), device_id_type=MESH,
            ))
            copies[-1].start()
        return copies

    def arrive(buf, ssem, rsem):
        for k in range(1, vocab):
            source = lax.rem(my_v + k, vocab)
            pltpu.make_async_remote_copy(
                src_ref=buf.at[source], dst_ref=buf.at[source],
                send_sem=ssem.at[k], recv_sem=rsem.at[source],
                device_id=(my_dp, source), device_id_type=MESH,
            ).wait_recv()

    stat_in[my_v, 0:depth, :] = tops
    stat_in[my_v, depth:2 * depth, :] = sums
    stat_copies = exchange(stat_in, stat_ssem, stat_rsem)

    lens_row = jnp.zeros((depth, LANES), jnp.int32)
    slots = []
    for n in range(seqs):
        lens_row = jnp.where(lane == n, lens[n], lens_row)
        rank = jnp.int32(0)
        for i in range(n):
            rank = rank + jnp.where(own[i] == own[n], 1, 0)
        slots.append(own[n] * capacity + rank)
    live = sub < lens_row
    rows = groups * capacity
    pick_row = lax.broadcasted_iota(jnp.int32, (rows, seqs), 0)
    pick_col = lax.broadcasted_iota(jnp.int32, (rows, seqs), 1)
    picker = jnp.zeros((rows, seqs), jnp.float32)
    for n in range(seqs):
        picker = jnp.where((pick_col == n) & (pick_row == slots[n]), 1.0, picker)
    picker = picker.astype(jnp.bfloat16)

    arrive(stat_in, stat_ssem, stat_rsem)
    peak_all = tops
    for p in range(vocab):
        peak_all = jnp.maximum(peak_all, stat_in[p, 0:depth, :])
    merged = zero
    for p in range(vocab):
        factor = jnp.where(lane < seqs, jnp.exp(stat_in[p, 0:depth, :] - peak_all), 1.0)
        merged = merged + stat_in[p, depth:2 * depth, :] * factor
    scale = jnp.exp(tops - peak_all) / merged

    excess_sum = zero
    for n in range(seqs):
        scale_n = jnp.broadcast_to(scale[:, n:n + 1], (depth, LANES))

        def gap(base, count, c, n=n, scale_n=scale_n):
            c = list(c)
            for k in range(count):
                place = (base + k, pl.ds(n * depth, depth), slice(None))
                target = e[place] * scale_n
                over = jnp.maximum(target - d[n, :, lane_tile(base + k)].astype(jnp.float32), 0.0)
                e[place] = over + mixing * target
                c[k % 4] = c[k % 4] + over
            return tuple(c)

        first = zero
        if tail:
            place = (full, pl.ds(n * depth, depth), slice(None))
            target = e[place] * scale_n
            first = jnp.maximum(target - tail_tile(d, n, 0.0), 0.0)
            e[place] = first + mixing * target
        c = sweep(0, full, gap, (first, zero, zero, zero))
        total = jnp.sum((c[0] + c[1]) + (c[2] + c[3]), axis=1, keepdims=True)
        excess_sum = jnp.where(lane == n, total, excess_sum)

    spread_in[my_v] = excess_sum
    spread_copies = exchange(spread_in, spr_ssem, spr_rsem)

    chosen = pltpu.roll(merged, LANES - seqs, 1)
    drafted = pltpu.roll(merged, LANES - 2 * seqs, 1)
    safe_draft = jnp.where(live, drafted, 1.0)
    accept = jnp.where(live, jnp.minimum(1.0, jnp.exp(chosen - peak_all) / merged / safe_draft), 0.0)
    before = []
    running = jnp.ones((1, LANES), jnp.float32)
    expected = jnp.zeros((1, LANES), jnp.float32)
    for j in range(depth):
        before.append(running)
        running = running * accept[j:j + 1, :]
        expected = expected + running
    before = jnp.concatenate(before, axis=0)
    weight = jnp.where(live, before * (1.0 - accept), 0.0)

    sent_accept = zero
    sent_expected = zero
    expected = jnp.broadcast_to(expected, (depth, LANES))
    for n in range(seqs):
        at_slot = lane == slots[n]
        sent_accept = jnp.where(at_slot, accept[:, n:n + 1], sent_accept)
        sent_expected = jnp.where(at_slot, expected[:, n:n + 1], sent_expected)
    for g in range(groups):
        shift = (LANES - g * capacity) % LANES
        small[g, 0:depth, :] = pltpu.roll(sent_accept, shift, 1) if shift else sent_accept
        small[g, depth:2 * depth, :] = pltpu.roll(sent_expected, shift, 1) if shift else sent_expected
    routed = []
    for k in range(1, groups):
        to = lax.rem(my_dp + k, groups)
        routed.append(pltpu.make_async_remote_copy(
            src_ref=small.at[to], dst_ref=small_out.at[my_dp],
            send_sem=sm_ssem.at[k], recv_sem=sm_rsem.at[my_dp],
            device_id=(to, my_v), device_id_type=MESH,
        ))
        routed[-1].start()
    own_copies = [pltpu.make_async_copy(small.at[my_dp], small_out.at[my_dp], local_sem.at[CHUNKS])]
    own_copies[0].start()

    arrive(spread_in, spr_ssem, spr_rsem)
    spread = spread_in[0]
    for p in range(1, vocab):
        spread = spread + spread_in[p]
    coef = weight / (spread + mixing)
    diag = lax.broadcasted_iota(jnp.int32, (seqs, LANES), 0) == lax.broadcasted_iota(jnp.int32, (seqs, LANES), 1)
    coefs = []
    for j in range(depth):
        row = jnp.where(diag, jnp.broadcast_to(coef[j:j + 1, :], (seqs, LANES)), 0.0)
        coefs.append(jnp.broadcast_to(jnp.sum(row, axis=1, keepdims=True), (seqs, LANES)))

    bounds = [tiles * c // CHUNKS for c in range(CHUNKS + 1)]
    for c in range(CHUNKS):
        def mix(base, count, carry):
            pieces = []
            for k in range(count):
                total = e[base + k, pl.ds(0, seqs, stride=depth), :] * coefs[0]
                for j in range(1, depth):
                    total = total + e[base + k, pl.ds(j, seqs, stride=depth), :] * coefs[j]
                pieces.append(total)
            mixed = pieces[0] if count == 1 else jnp.concatenate(pieces, axis=1)
            sent = jnp.dot(picker, mixed.astype(jnp.bfloat16), preferred_element_type=jnp.float32)
            columns = pl.ds(pl.multiple_of(base * LANES, LANES), count * LANES)
            for g in range(groups):
                send[g, :, columns] = sent[g * capacity:(g + 1) * capacity, :].astype(jnp.bfloat16)
            return carry

        sweep(bounds[c], bounds[c + 1], mix, 0)
        columns = pl.ds(bounds[c] * LANES, (bounds[c + 1] - bounds[c]) * LANES)
        for k in range(1, groups):
            to = lax.rem(my_dp + k, groups)
            routed.append(pltpu.make_async_remote_copy(
                src_ref=send.at[to, :, columns], dst_ref=out.at[my_dp, :, columns],
                send_sem=out_ssem.at[c, k], recv_sem=out_rsem.at[c, my_dp],
                device_id=(to, my_v), device_id_type=MESH,
            ))
            routed[-1].start()
        own_copies.append(pltpu.make_async_copy(
            send.at[my_dp, :, columns], out.at[my_dp, :, columns], local_sem.at[c]))
        own_copies[-1].start()

    for k in range(1, groups):
        source = lax.rem(my_dp + k, groups)
        pltpu.make_async_remote_copy(
            src_ref=small.at[source], dst_ref=small_out.at[source],
            send_sem=sm_ssem.at[k], recv_sem=sm_rsem.at[source],
            device_id=(source, my_v), device_id_type=MESH,
        ).wait_recv()
    for c in range(CHUNKS):
        columns = pl.ds(bounds[c] * LANES, (bounds[c + 1] - bounds[c]) * LANES)
        for k in range(1, groups):
            source = lax.rem(my_dp + k, groups)
            pltpu.make_async_remote_copy(
                src_ref=send.at[source, :, columns], dst_ref=out.at[source, :, columns],
                send_sem=out_ssem.at[c, k], recv_sem=out_rsem.at[c, source],
                device_id=(source, my_v), device_id_type=MESH,
            ).wait_recv()
    for copy in own_copies:
        copy.wait()
    for copy in stat_copies + spread_copies + routed:
        copy.wait_send()


def body(logits, draft_probs, draft_tokens, draft_lengths, owner_group):
    groups = lax.axis_size("dp")
    vocab = lax.axis_size("vocab")
    seqs, depth, width = logits.shape
    capacity = max(2, 2 * seqs // groups)
    tiles = -(-width // LANES)
    padded = tiles * LANES
    smem = pl.BlockSpec(memory_space=pltpu.SMEM)
    hbm = pl.BlockSpec(memory_space=pl.ANY)
    dma = pltpu.SemaphoreType.DMA
    out, small = pl.pallas_call(
        functools.partial(kernel, (groups, vocab, capacity)),
        out_shape=(
            jax.ShapeDtypeStruct((groups, capacity, padded), jnp.bfloat16),
            jax.ShapeDtypeStruct((groups, 2 * depth, LANES), jnp.float32),
        ),
        in_specs=[smem, smem, smem, hbm, hbm],
        out_specs=(hbm, hbm),
        scratch_shapes=[
            pltpu.VMEM((seqs, depth, width), jnp.bfloat16),
            pltpu.VMEM((seqs, depth, width), jnp.bfloat16),
            pltpu.VMEM((tiles, seqs * depth, LANES), jnp.float32),
            pltpu.VMEM((groups, capacity, padded), jnp.bfloat16),
            pltpu.VMEM((vocab, 2 * depth, LANES), jnp.float32),
            pltpu.VMEM((vocab, depth, LANES), jnp.float32),
            pltpu.VMEM((groups, 2 * depth, LANES), jnp.float32),
            dma((2 * seqs,)),
            dma((vocab,)),
            dma((vocab,)),
            dma((vocab,)),
            dma((vocab,)),
            dma((CHUNKS, groups)),
            dma((CHUNKS, groups)),
            dma((groups,)),
            dma((groups,)),
            dma((CHUNKS + 1,)),
        ],
        compiler_params=pltpu.CompilerParams(collective_id=0, has_side_effects=True),
    )(draft_tokens, draft_lengths, owner_group, logits, draft_probs)
    correction = out[:, :, :width].reshape(groups * capacity, width)
    accept_ratio = small[:, :depth, :capacity].transpose(0, 2, 1).reshape(groups * capacity, depth)
    expected_accepted = small[:, depth, :capacity].reshape(groups * capacity)
    return (correction, accept_ratio, expected_accepted)


def solution(mesh):
    placed = (P("dp", None, "vocab"), P("dp", None, "vocab"), P("dp", None), P("dp"), P("dp"))
    return jax.shard_map(
        body,
        mesh=mesh,
        in_specs=placed,
        out_specs=(P("dp", "vocab"), P("dp", None), P("dp")),
        check_vma=False,
    )
```

time: 99.2 us -> 38.1 us (0.38)
  blocking collectives: 57.6 us -> 0 us
  Pallas kernels: 0 us -> 32.2 us
  other arithmetic: 15.6 us -> 0 us
  starting transfers between devices: 11.4 us -> 0 us
  waiting for transfers between devices: 7.9 us -> 0 us
    psum x2 -> x0, blocking collectives: 39.5 us -> none  [the longest x1 25.9 us: verify(): spread = lax.psum(jnp.sum(excess, axis=2), 'vocab')]
    pallas_call x0 -> x1, Pallas kernels: none -> 32.2 us  [body(): pl.pallas_call(functools.partial(kernel, (groups, vocab, capacity)), out_...]
    pmax x1 -> x0, blocking collectives: 18.1 us -> none  [verify(): top = lax.pmax(jnp.max(scores, axis=2), 'vocab')]
    reduce_sum x7 -> x0, other arithmetic: 11.7 us -> none  [the longest x1 4.79 us: verify(): jnp.sum(weight[:, :, None] * residual, axis=1).astype(jnp.bfloat16)]
    all_to_all x3 -> x0, starting transfers between devices: 11.4 us -> none  [the longest x1 4.2 us: body(): lax.all_to_all(sent_accept, 'dp', split_axis=0, concat_axis=0, tiled=True)]
    all_to_all x3 -> x0, waiting for transfers between devices: 7.9 us -> none  [the longest x1 4.61 us: body(): lax.all_to_all(outgoing, 'dp', split_axis=0, concat_axis=0, tiled=True)]
    all_to_all x5 -> x0, local copies, waits for them, and re-layouts: 3.82 us -> none  [the longest x2 2.04 us: body(): lax.all_to_all(outgoing, 'dp', split_axis=0, concat_axis=0, tiled=True)]
    reduce_max x1 -> x0, other arithmetic: 2.17 us -> none  [verify(): top = lax.pmax(jnp.max(scores, axis=2), 'vocab')]
  transfers between devices with their start and end apart: 3 -> 0, of which waited for: 2 -> 0; matrix products, arithmetic and copies ran while one was open for 8% -> 0% of each run, Pallas kernels for 0% -> 0%
where the time goes in v1:
time: 38.1 us; the launch traced here: 37.8 us
  Pallas kernels  32.2 us (85%)
  local copies, waits for them, and re-layouts  4.97 us (13%)
  between operations  0.64 us (2%)
    pallas_call x1, Pallas kernels, body(): pl.pallas_call(functools.partial(kernel, (groups, vocab, capacity)), out_...  32.2 us
    reshape x1, local copies, waits for them, and re-layouts, body(): correction = out[:, :, :width].reshape(groups * capacity, width)  2.15 us
    transpose x2, local copies, waits for them, and re-layouts, body(): small[:, :depth, :capacity].transpose(0, 2, 1)  0.82 us

profile of v1, /device:TPU:0, one launch (start us, length us, event | category | flops | bytes accessed | tf_op | source)
XLA Modules:
  0.0 37.8 jit_solution(13442590066666076038)
XLA Ops:
  0.6 32.2 %shard_map.76 = (bf16[4,4,19072]{2,1,0:T(4,128)(2,1)}, f32[4,16,128]{2,1,0:T(8,128)}) custom-call(s32[8,8]{1,0:T(8,128)} %tok.1, s32[8]{0:T(128)} %lens.1, s32[8]{0:T(128)} %own.1, bf16[8,8,19008]{2,1,0:T(8,128)(2,1)} %x_hbm.1, bf16[8,8,19008]{2,1,0:T(8,128)(2,1)} %d_hbm.1), custom_call_target="tpu_custom_call" | custom-call | tf_op jit(solution)/shard_map/pallas_call | solution.py:320
  32.8 0.7 %slice_bitcast_fusion = f32[4,4,8]{1,2,0:T(8,128)S(1)} fusion(f32[4,16,128]{2,1,0:T(8,128)} %get-tuple-element.6), kind=kLoop, calls=%fused_computation | loop fusion | bytes 1024 | tf_op jit(solution)/shard_map/transpose | solution.py:350
  33.5 0.1 copy.8
  33.6 0.7 %copy.9 = f32[16,8]{0,1:T(8,128)} copy(f32[16,8]{1,0:T(8,128)S(1)} %bitcast.5) | data formatting | bytes 1024
  34.3 0.7 %slice_reduce_fusion = f32[4,4]{1,0:T(4,128)S(1)} fusion(f32[4,16,128]{2,1,0:T(8,128)} %get-tuple-element.6), kind=kLoop, calls=%fused_computation.1 | loop fusion | bytes 128 | tf_op jit(solution)/shard_map/slice | solution.py:351
  35.0 0.6 %reshape_squeeze.3 = f32[16]{0:T(128)} reshape(f32[4,4]{1,0:T(4,128)S(1)} %slice_reduce_fusion) | data formatting | bytes 128 | tf_op jit(solution)/shard_map/reshape;squeeze | solution.py:351
  35.6 2.2 %reshape.12 = bf16[16,19008]{1,0:T(8,128)(2,1)} reshape(bf16[4,4,19008]{2,1,0:T(4,128)(2,1)} %bitcast.4) | data formatting | bytes 1216512 | tf_op jit(solution)/shard_map/reshape | solution.py:349

commit v2 on v1

--- a/solution.py
+++ b/solution.py
@@ -9,24 +9,27 @@
 
 mixing = 0.1
 LANES = 128
-GROUP = 8
-CHUNKS = 4
+GROUP = 40
+MIX_GROUP = 8
+CHUNKS = 5
 LOW = -1e30
 MESH = pl.DeviceIdType.MESH
 
 
-def sweep(start, stop, fn, carry):
-    whole = (stop - start) // GROUP
+def sweep(start, stop, fn, carry, most=GROUP):
+    extent = stop - start
+    size = max(1, min(most, extent))
+    size = min(range(max(1, size // 2), size + 1), key=lambda g: (extent % g, -g))
+    whole = extent // size
 
     def step(i, c):
-        base = start + i * GROUP
-        return fn(base, GROUP, c)
+        return fn(start + i * size, size, c)
 
     if whole:
         carry = lax.fori_loop(0, whole, step, carry)
-    rest = (stop - start) % GROUP
+    rest = extent % size
     if rest:
-        carry = fn(start + whole * GROUP, rest, carry)
+        carry = fn(start + whole * size, rest, carry)
     return carry
 
 
@@ -37,9 +40,9 @@
 def kernel(
     dims,
     tok, lens, own, x_hbm, d_hbm,
-    out, small_out,
-    x, d, e, send, stat_in, spread_in, small,
-    load_sem, stat_ssem, stat_rsem, spr_ssem, spr_rsem, out_ssem, out_rsem, sm_ssem, sm_rsem, local_sem,
+    out, accept_out, expected_out,
+    x, d, e, send, landed, block, stat_in, spread_in, small, small_in,
+    load_sem, stat_ssem, stat_rsem, spr_ssem, spr_rsem, out_ssem, out_rsem, sm_ssem, sm_rsem, local_sem, store_sem,
 ):
     groups, vocab, capacity = dims
     seqs, depth, width = x_hbm.shape
@@ -76,13 +79,8 @@
 
     tops = zero
     sums = zero
-    column0 = my_v * width
     for n in range(seqs):
         loads[n].wait()
-        spot = jnp.zeros((depth, LANES), jnp.int32)
-        for j in range(depth):
-            spot = jnp.where(sub == j, tok[n, j], spot)
-        spot = spot - column0 - lane
 
         def peak(base, count, c, n=n):
             c = list(c)
@@ -95,36 +93,25 @@
         top = jnp.maximum(jnp.maximum(c[0], c[1]), jnp.maximum(c[2], c[3]))
         top = jnp.broadcast_to(jnp.max(top, axis=1, keepdims=True), (depth, LANES))
 
-        loads[seqs + n].wait()
-
-        def expo(base, count, c, n=n, top=top, spot=spot):
+        def expo(base, count, c, n=n, top=top):
             c = list(c)
             for k in range(count):
                 raw = x[n, :, lane_tile(base + k)].astype(jnp.float32)
                 value = jnp.exp(raw - top)
                 e[base + k, pl.ds(n * depth, depth), :] = value
                 c[k % 4] = c[k % 4] + value
-                hit = spot == (base + k) * LANES
-                c[4] = jnp.where(hit, raw, c[4])
-                c[5] = jnp.where(hit, d[n, :, lane_tile(base + k)].astype(jnp.float32), c[5])
             return tuple(c)
 
         first = zero
-        picked_x = zero
-        picked_d = zero
         if tail:
             raw = tail_tile(x, n, LOW)
             first = jnp.exp(raw - top)
             e[full, pl.ds(n * depth, depth), :] = first
-            hit = (spot == full * LANES) & (lane < tail)
-            picked_x = jnp.where(hit, raw, zero)
-            picked_d = jnp.where(hit, tail_tile(d, n, 0.0), zero)
-        c = sweep(0, full, expo, (first, zero, zero, zero, picked_x, picked_d))
+        c = sweep(0, full, expo, (first, zero, zero, zero))
         total = jnp.sum((c[0] + c[1]) + (c[2] + c[3]), axis=1, keepdims=True)
-        tops = jnp.where(lax.rem(lane, seqs) == n, top, tops)
+        tops = jnp.where(lane == n, top, tops)
         sums = jnp.where(lane == n, total, sums)
-        sums = jnp.where(lane == seqs + n, jnp.sum(c[4], axis=1, keepdims=True), sums)
-        sums = jnp.where(lane == 2 * seqs + n, jnp.sum(c[5], axis=1, keepdims=True), sums)
+        sums = jnp.where(lane == seqs + n, top, sums)
 
     pl.semaphore_wait(barrier, vocab - 1 + groups - 1)
 
@@ -149,8 +136,7 @@
                 device_id=(my_dp, source), device_id_type=MESH,
             ).wait_recv()
 
-    stat_in[my_v, 0:depth, :] = tops
-    stat_in[my_v, depth:2 * depth, :] = sums
+    stat_in[my_v] = sums
     stat_copies = exchange(stat_in, stat_ssem, stat_rsem)
 
     lens_row = jnp.zeros((depth, LANES), jnp.int32)
@@ -170,17 +156,40 @@
         picker = jnp.where((pick_col == n) & (pick_row == slots[n]), 1.0, picker)
     picker = picker.astype(jnp.bfloat16)
 
+    column0 = my_v * width
+    excess_sum = zero
+    for n in range(seqs):
+        loads[seqs + n].wait()
+        spot = jnp.zeros((depth, LANES), jnp.int32)
+        for j in range(depth):
+            spot = jnp.where(sub == j, tok[n, j], spot)
+        spot = spot - column0 - lane
+
+        def pick(base, count, c, n=n, spot=spot):
+            c = list(c)
+            for k in range(count):
+                hit = spot == (base + k) * LANES
+                c[0] = jnp.where(hit, x[n, :, lane_tile(base + k)].astype(jnp.float32), c[0])
+                c[1] = jnp.where(hit, d[n, :, lane_tile(base + k)].astype(jnp.float32), c[1])
+            return tuple(c)
+
+        first = (zero, zero)
+        if tail:
+            hit = (spot == full * LANES) & (lane < tail)
+            first = (jnp.where(hit, tail_tile(x, n, 0.0), zero), jnp.where(hit, tail_tile(d, n, 0.0), zero))
+        c = sweep(0, full, pick, first)
+        excess_sum = jnp.where(lane == seqs + n, jnp.sum(c[0], axis=1, keepdims=True), excess_sum)
+        excess_sum = jnp.where(lane == 2 * seqs + n, jnp.sum(c[1], axis=1, keepdims=True), excess_sum)
+
     arrive(stat_in, stat_ssem, stat_rsem)
-    peak_all = tops
-    for p in range(vocab):
-        peak_all = jnp.maximum(peak_all, stat_in[p, 0:depth, :])
+    parts = [stat_in[p] for p in range(vocab)]
+    peaks = [pltpu.roll(part, LANES - seqs, 1) for part in parts]
+    peak_all = functools.reduce(jnp.maximum, peaks)
     merged = zero
-    for p in range(vocab):
-        factor = jnp.where(lane < seqs, jnp.exp(stat_in[p, 0:depth, :] - peak_all), 1.0)
-        merged = merged + stat_in[p, depth:2 * depth, :] * factor
+    for part, local_peak in zip(parts, peaks):
+        merged = merged + part * jnp.exp(local_peak - peak_all)
     scale = jnp.exp(tops - peak_all) / merged
 
-    excess_sum = zero
     for n in range(seqs):
         scale_n = jnp.broadcast_to(scale[:, n:n + 1], (depth, LANES))
 
@@ -207,8 +216,12 @@
     spread_in[my_v] = excess_sum
     spread_copies = exchange(spread_in, spr_ssem, spr_rsem)
 
-    chosen = pltpu.roll(merged, LANES - seqs, 1)
-    drafted = pltpu.roll(merged, LANES - 2 * seqs, 1)
+    arrive(spread_in, spr_ssem, spr_rsem)
+    spread = spread_in[0]
+    for p in range(1, vocab):
+        spread = spread + spread_in[p]
+    chosen = pltpu.roll(spread, LANES - seqs, 1)
+    drafted = pltpu.roll(spread, LANES - 2 * seqs, 1)
     safe_draft = jnp.where(live, drafted, 1.0)
     accept = jnp.where(live, jnp.minimum(1.0, jnp.exp(chosen - peak_all) / merged / safe_draft), 0.0)
     before = []
@@ -221,33 +234,6 @@
     before = jnp.concatenate(before, axis=0)
     weight = jnp.where(live, before * (1.0 - accept), 0.0)
 
-    sent_accept = zero
-    sent_expected = zero
-    expected = jnp.broadcast_to(expected, (depth, LANES))
-    for n in range(seqs):
-        at_slot = lane == slots[n]
-        sent_accept = jnp.where(at_slot, accept[:, n:n + 1], sent_accept)
-        sent_expected = jnp.where(at_slot, expected[:, n:n + 1], sent_expected)
-    for g in range(groups):
-        shift = (LANES - g * capacity) % LANES
-        small[g, 0:depth, :] = pltpu.roll(sent_accept, shift, 1) if shift else sent_accept
-        small[g, depth:2 * depth, :] = pltpu.roll(sent_expected, shift, 1) if shift else sent_expected
-    routed = []
-    for k in range(1, groups):
-        to = lax.rem(my_dp + k, groups)
-        routed.append(pltpu.make_async_remote_copy(
-            src_ref=small.at[to], dst_ref=small_out.at[my_dp],
-            send_sem=sm_ssem.at[k], recv_sem=sm_rsem.at[my_dp],
-            device_id=(to, my_v), device_id_type=MESH,
-        ))
-        routed[-1].start()
-    own_copies = [pltpu.make_async_copy(small.at[my_dp], small_out.at[my_dp], local_sem.at[CHUNKS])]
-    own_copies[0].start()
-
-    arrive(spread_in, spr_ssem, spr_rsem)
-    spread = spread_in[0]
-    for p in range(1, vocab):
-        spread = spread + spread_in[p]
     coef = weight / (spread + mixing)
     diag = lax.broadcasted_iota(jnp.int32, (seqs, LANES), 0) == lax.broadcasted_iota(jnp.int32, (seqs, LANES), 1)
     coefs = []
@@ -255,6 +241,8 @@
         row = jnp.where(diag, jnp.broadcast_to(coef[j:j + 1, :], (seqs, LANES)), 0.0)
         coefs.append(jnp.broadcast_to(jnp.sum(row, axis=1, keepdims=True), (seqs, LANES)))
 
+    routed = []
+    own_copies = []
     bounds = [tiles * c // CHUNKS for c in range(CHUNKS + 1)]
     for c in range(CHUNKS):
         def mix(base, count, carry):
@@ -271,37 +259,77 @@
                 send[g, :, columns] = sent[g * capacity:(g + 1) * capacity, :].astype(jnp.bfloat16)
             return carry
 
-        sweep(bounds[c], bounds[c + 1], mix, 0)
+        sweep(bounds[c], bounds[c + 1], mix, 0, MIX_GROUP)
         columns = pl.ds(bounds[c] * LANES, (bounds[c + 1] - bounds[c]) * LANES)
         for k in range(1, groups):
             to = lax.rem(my_dp + k, groups)
             routed.append(pltpu.make_async_remote_copy(
-                src_ref=send.at[to, :, columns], dst_ref=out.at[my_dp, :, columns],
+                src_ref=send.at[to, :, columns], dst_ref=landed.at[my_dp, :, columns],
                 send_sem=out_ssem.at[c, k], recv_sem=out_rsem.at[c, my_dp],
                 device_id=(to, my_v), device_id_type=MESH,
             ))
             routed[-1].start()
         own_copies.append(pltpu.make_async_copy(
-            send.at[my_dp, :, columns], out.at[my_dp, :, columns], local_sem.at[c]))
+            send.at[my_dp, :, columns], landed.at[my_dp, :, columns], local_sem.at[c]))
         own_copies[-1].start()
 
+    sent_accept = zero
+    sent_expected = zero
+    expected = jnp.broadcast_to(expected, (depth, LANES))
+    for n in range(seqs):
+        at_slot = lane == slots[n]
+        sent_accept = jnp.where(at_slot, accept[:, n:n + 1], sent_accept)
+        sent_expected = jnp.where(at_slot, expected[:, n:n + 1], sent_expected)
+    for g in range(groups):
+        shift = (LANES - g * capacity) % LANES
+        small[g, 0:depth, :] = pltpu.roll(sent_accept, shift, 1) if shift else sent_accept
+        small[g, depth:2 * depth, :] = pltpu.roll(sent_expected, shift, 1) if shift else sent_expected
     for k in range(1, groups):
-        source = lax.rem(my_dp + k, groups)
-        pltpu.make_async_remote_copy(
-            src_ref=small.at[source], dst_ref=small_out.at[source],
-            send_sem=sm_ssem.at[k], recv_sem=sm_rsem.at[source],
-            device_id=(source, my_v), device_id_type=MESH,
-        ).wait_recv()
+        to = lax.rem(my_dp + k, groups)
+        routed.append(pltpu.make_async_remote_copy(
+            src_ref=small.at[to], dst_ref=small_in.at[my_dp],
+            send_sem=sm_ssem.at[k], recv_sem=sm_rsem.at[my_dp],
+            device_id=(to, my_v), device_id_type=MESH,
+        ))
+        routed[-1].start()
+    stores = []
     for c in range(CHUNKS):
         columns = pl.ds(bounds[c] * LANES, (bounds[c + 1] - bounds[c]) * LANES)
         for k in range(1, groups):
             source = lax.rem(my_dp + k, groups)
             pltpu.make_async_remote_copy(
-                src_ref=send.at[source, :, columns], dst_ref=out.at[source, :, columns],
+                src_ref=send.at[source, :, columns], dst_ref=landed.at[source, :, columns],
                 send_sem=out_ssem.at[c, k], recv_sem=out_rsem.at[c, source],
                 device_id=(source, my_v), device_id_type=MESH,
             ).wait_recv()
-    for copy in own_copies:
+        own_copies[c].wait()
+
+        def gather(base, count, carry):
+            span = pl.ds(pl.multiple_of(base * LANES, LANES), count * LANES)
+            pieces = [landed[g, :, span].astype(jnp.float32) for g in range(groups)]
+            block[:, span] = jnp.concatenate(pieces, axis=0).astype(jnp.bfloat16)
+            return carry
+
+        sweep(bounds[c], bounds[c + 1], gather, 0, MIX_GROUP)
+        stores.append(pltpu.make_async_copy(block.at[:, columns], out.at[:, columns], store_sem.at[c]))
+        stores[-1].start()
+    small_in[my_dp] = small[my_dp]
+    for k in range(1, groups):
+        source = lax.rem(my_dp + k, groups)
+        pltpu.make_async_remote_copy(
+            src_ref=small.at[source], dst_ref=small_in.at[source],
+            send_sem=sm_ssem.at[k], recv_sem=sm_rsem.at[source],
+            device_id=(source, my_v), device_id_type=MESH,
+        ).wait_recv()
+    final_accept = zero
+    final_expected = zero
+    for g in range(groups):
+        mine = (lane >= g * capacity) & (lane < (g + 1) * capacity)
+        final_accept = jnp.where(mine, pltpu.roll(small_in[g, 0:depth, :], g * capacity, 1), final_accept)
+        final_expected = jnp.where(mine, pltpu.roll(small_in[g, depth:2 * depth, :], g * capacity, 1), final_expected)
+    accept_out[...] = final_accept[:, :rows]
+    expected_out[...] = final_expected[0:1, :rows]
+    for copy in stores:
         copy.wait()
     for copy in stat_copies + spread_copies + routed:
         copy.wait_send()
@@ -317,21 +345,27 @@
     smem = pl.BlockSpec(memory_space=pltpu.SMEM)
     hbm = pl.BlockSpec(memory_space=pl.ANY)
     dma = pltpu.SemaphoreType.DMA
-    out, small = pl.pallas_call(
+    slots = groups * capacity
+    vmem = pl.BlockSpec(memory_space=pltpu.VMEM)
+    out, accept, expected = pl.pallas_call(
         functools.partial(kernel, (groups, vocab, capacity)),
         out_shape=(
-            jax.ShapeDtypeStruct((groups, capacity, padded), jnp.bfloat16),
-            jax.ShapeDtypeStruct((groups, 2 * depth, LANES), jnp.float32),
+            jax.ShapeDtypeStruct((slots, padded), jnp.bfloat16),
+            jax.ShapeDtypeStruct((depth, slots), jnp.float32),
+            jax.ShapeDtypeStruct((1, slots), jnp.float32),
         ),
         in_specs=[smem, smem, smem, hbm, hbm],
-        out_specs=(hbm, hbm),
+        out_specs=(hbm, vmem, vmem),
         scratch_shapes=[
             pltpu.VMEM((seqs, depth, width), jnp.bfloat16),
             pltpu.VMEM((seqs, depth, width), jnp.bfloat16),
             pltpu.VMEM((tiles, seqs * depth, LANES), jnp.float32),
             pltpu.VMEM((groups, capacity, padded), jnp.bfloat16),
-            pltpu.VMEM((vocab, 2 * depth, LANES), jnp.float32),
+            pltpu.VMEM((groups, capacity, padded), jnp.bfloat16),
+            pltpu.VMEM((slots, padded), jnp.bfloat16),
             pltpu.VMEM((vocab, depth, LANES), jnp.float32),
+            pltpu.VMEM((vocab, depth, LANES), jnp.float32),
+            pltpu.VMEM((groups, 2 * depth, LANES), jnp.float32),
             pltpu.VMEM((groups, 2 * depth, LANES), jnp.float32),
             dma((2 * seqs,)),
             dma((vocab,)),
@@ -342,13 +376,14 @@
             dma((CHUNKS, groups)),
             dma((groups,)),
             dma((groups,)),
-            dma((CHUNKS + 1,)),
+            dma((CHUNKS,)),
+            dma((CHUNKS,)),
         ],
         compiler_params=pltpu.CompilerParams(collective_id=0, has_side_effects=True),
     )(draft_tokens, draft_lengths, owner_group, logits, draft_probs)
-    correction = out[:, :, :width].reshape(groups * capacity, width)
-    accept_ratio = small[:, :depth, :capacity].transpose(0, 2, 1).reshape(groups * capacity, depth)
-    expected_accepted = small[:, depth, :capacity].reshape(groups * capacity)
+    correction = out[:, :width]
+    accept_ratio = accept.T
+    expected_accepted = expected.reshape(slots)
     return (correction, accept_ratio, expected_accepted)
 
 

time: 38.1 us -> 35.6 us (0.934)
  Pallas kernels: 32.2 us -> 30.4 us
  local copies, waits for them, and re-layouts: 4.97 us -> 4.32 us
    unnamed x1 -> x3, local copies, waits for them, and re-layouts: 0.66 us -> 4.32 us
    reshape x1 -> x0, local copies, waits for them, and re-layouts: 2.15 us -> none  [body(): correction = out[:, :, :width].reshape(groups * capacity, width)]
    pallas_call x1, Pallas kernels: 32.2 us -> 30.4 us  [body(): pl.pallas_call(functools.partial(kernel, (groups, vocab, capacity)), out_...]
    transpose x2 -> x0, local copies, waits for them, and re-layouts: 0.82 us -> none  [body(): small[:, :depth, :capacity].transpose(0, 2, 1)]
    slice x1 -> x0, local copies, waits for them, and re-layouts: 0.74 us -> none  [body(): expected_accepted = small[:, depth, :capacity].reshape(groups * capacity)]
    another operation x1 -> x0, local copies, waits for them, and re-layouts: 0.6 us -> none  [body(): expected_accepted = small[:, depth, :capacity].reshape(groups * capacity)]
where the time goes in v2:
time: 35.6 us; the launch traced here: 35.4 us
  Pallas kernels  30.4 us (85%)
  local copies, waits for them, and re-layouts  4.32 us (12%)
  between operations  0.64 us (2%)
    pallas_call x1, Pallas kernels, body(): pl.pallas_call(functools.partial(kernel, (groups, vocab, capacity)), out_...  30.4 us
    unnamed x3, local copies, waits for them, and re-layouts  4.32 us

profile of v2, /device:TPU:0, one launch (start us, length us, event | category | flops | bytes accessed | tf_op | source)
XLA Modules:
  0.0 35.4 jit_solution(7661148951084648566)
XLA Ops:
  0.6 30.4 %shard_map.76 = (bf16[16,19072]{1,0:T(8,128)(2,1)}, f32[8,16]{1,0:T(8,128)}, f32[1,16]{1,0:T(1,128)}) custom-call(s32[8,8]{1,0:T(8,128)} %tok.1, s32[8]{0:T(128)} %lens.1, s32[8]{0:T(128)} %own.1, bf16[8,8,19008]{2,1,0:T(8,128)(2,1)} %x_hbm.1, bf16[8,8,19008]{2,1,0:T(8,128)(2,1)} %d_hbm.1), custom_call_target="tpu_custom_call" | custom-call | tf_op jit(solution)/shard_map/pallas_call | solution.py:350
  31.0 1.9 %copy.11 = bf16[16,19008]{1,0:T(8,128)(2,1)} copy(bf16[16,19008]{1,0:T(8,128)(2,1)} %bitcast.3) | data formatting | bytes 1216512
  33.0 1.3 %copy.12 = f32[16,8]{0,1:T(8,128)} copy(f32[16,8]{0,1:T(8,128)} %bitcast.4) | data formatting | bytes 1024
  34.2 1.1 %copy.13 = f32[16]{0:T(128)} copy(f32[16]{0:T(128)} %bitcast.5) | data formatting | bytes 128

commit v3 on v2

--- a/solution.py
+++ b/solution.py
@@ -39,10 +39,10 @@
 
 def kernel(
     dims,
-    tok, lens, own, x_hbm, d_hbm,
+    tok_hbm, lens_hbm, own_hbm, x_hbm, d_hbm,
     out, accept_out, expected_out,
-    x, d, e, send, landed, block, stat_in, spread_in, small, small_in,
-    load_sem, stat_ssem, stat_rsem, spr_ssem, spr_rsem, out_ssem, out_rsem, sm_ssem, sm_rsem, local_sem, store_sem,
+    tok, lens, own, x, d, e, send, landed, block, stat_in, spread_in, small, small_in,
+    scalar_sem, load_sem, stat_ssem, stat_rsem, spr_ssem, spr_rsem, out_ssem, out_rsem, sm_ssem, sm_rsem, local_sem, store_sem,
 ):
     groups, vocab, capacity = dims
     seqs, depth, width = x_hbm.shape
@@ -59,7 +59,10 @@
         loads.append(pltpu.make_async_copy(d_hbm.at[n], d.at[n], load_sem.at[seqs + n]))
     for n in range(seqs):
         loads[n].start()
-        loads[seqs + n].start()
+    scalars = []
+    for i, (source, target) in enumerate(((tok_hbm, tok), (lens_hbm, lens), (own_hbm, own))):
+        scalars.append(pltpu.make_async_copy(source, target, scalar_sem.at[i]))
+        scalars[-1].start()
 
     barrier = pltpu.get_barrier_semaphore()
     v_peers = [lax.rem(my_v + k, vocab) for k in range(1, vocab)]
@@ -81,6 +84,7 @@
     sums = zero
     for n in range(seqs):
         loads[n].wait()
+        loads[seqs + n].start()
 
         def peak(base, count, c, n=n):
             c = list(c)
@@ -138,6 +142,9 @@
 
     stat_in[my_v] = sums
     stat_copies = exchange(stat_in, stat_ssem, stat_rsem)
+
+    for copy in scalars:
+        copy.wait()
 
     lens_row = jnp.zeros((depth, LANES), jnp.int32)
     slots = []
@@ -342,8 +349,8 @@
     capacity = max(2, 2 * seqs // groups)
     tiles = -(-width // LANES)
     padded = tiles * LANES
-    smem = pl.BlockSpec(memory_space=pltpu.SMEM)
-    hbm = pl.BlockSpec(memory_space=pl.ANY)
+    anywhere = pl.BlockSpec(memory_space=pl.ANY)
+    hbm = pl.BlockSpec(memory_space=pltpu.HBM)
     dma = pltpu.SemaphoreType.DMA
     slots = groups * capacity
     vmem = pl.BlockSpec(memory_space=pltpu.VMEM)
@@ -354,9 +361,12 @@
             jax.ShapeDtypeStruct((depth, slots), jnp.float32),
             jax.ShapeDtypeStruct((1, slots), jnp.float32),
         ),
-        in_specs=[smem, smem, smem, hbm, hbm],
-        out_specs=(hbm, vmem, vmem),
+        in_specs=[hbm] * 5,
+        out_specs=(anywhere, vmem, vmem),
         scratch_shapes=[
+            pltpu.SMEM((seqs, depth), jnp.int32),
+            pltpu.SMEM((seqs,), jnp.int32),
+            pltpu.SMEM((seqs,), jnp.int32),
             pltpu.VMEM((seqs, depth, width), jnp.bfloat16),
             pltpu.VMEM((seqs, depth, width), jnp.bfloat16),
             pltpu.VMEM((tiles, seqs * depth, LANES), jnp.float32),
@@ -367,6 +377,7 @@
             pltpu.VMEM((vocab, depth, LANES), jnp.float32),
             pltpu.VMEM((groups, 2 * depth, LANES), jnp.float32),
             pltpu.VMEM((groups, 2 * depth, LANES), jnp.float32),
+            dma((3,)),
             dma((2 * seqs,)),
             dma((vocab,)),
             dma((vocab,)),
@@ -379,7 +390,9 @@
             dma((CHUNKS,)),
             dma((CHUNKS,)),
         ],
-        compiler_params=pltpu.CompilerParams(collective_id=0, has_side_effects=True),
+        compiler_params=pltpu.CompilerParams(
+            collective_id=0, has_side_effects=True, vmem_limit_bytes=54500 * 1024
+        ),
     )(draft_tokens, draft_lengths, owner_group, logits, draft_probs)
     correction = out[:, :width]
     accept_ratio = accept.T

time: 35.6 us -> 33.7 us (0.947)
  Pallas kernels: 30.4 us -> 28.9 us
  local copies, waits for them, and re-layouts: 4.32 us -> 3.92 us
    pallas_call x1, Pallas kernels: 30.4 us -> 28.9 us  [body(): pl.pallas_call(functools.partial(kernel, (groups, vocab, capacity)), out_...]
    unnamed x3 -> x9, local copies, waits for them, and re-layouts: 4.32 us -> 3.92 us
where the time goes in v3:
time: 33.7 us; the launch traced here: 33.5 us
  Pallas kernels  28.9 us (86%)
  local copies, waits for them, and re-layouts  3.92 us (12%)
  between operations  0.65 us (2%)
    pallas_call x1, Pallas kernels, body(): pl.pallas_call(functools.partial(kernel, (groups, vocab, capacity)), out_...  28.9 us
    unnamed x9, local copies, waits for them, and re-layouts  3.92 us

profile of v3, /device:TPU:0, one launch (start us, length us, event | category | flops | bytes accessed | tf_op | source)
XLA Modules:
  0.0 33.5 jit_solution(1574349809148313866)
XLA Ops:
  0.6 0.0 copy-start
  0.6 0.7 %copy-done = s32[8,8]{1,0:T(8,128)S(1)} copy-done((s32[8,8]{1,0:T(8,128)S(1)}, s32[8,8]{1,0:T(8,128)}, u32[]{:S(2)}) %copy-start) | copy-done | bytes 280
  1.3 0.0 copy-start.1
  1.3 0.7 %copy-done.1 = s32[8]{0:T(128)S(1)} copy-done((s32[8]{0:T(128)S(1)}, s32[8]{0:T(128)}, u32[]{:S(2)}) %copy-start.1) | copy-done | bytes 56
  2.0 0.0 copy-start.2
  2.0 0.7 %copy-done.2 = s32[8]{0:T(128)S(1)} copy-done((s32[8]{0:T(128)S(1)}, s32[8]{0:T(128)}, u32[]{:S(2)}) %copy-start.2) | copy-done | bytes 56
  2.6 28.9 %shard_map.76 = (bf16[16,19072]{1,0:T(8,128)(2,1)S(1)}, f32[8,16]{1,0:T(8,128)S(1)}, f32[1,16]{1,0:T(1,128)S(1)}) custom-call(s32[8,8]{1,0:T(8,128)S(1)} %copy-done, s32[8]{0:T(128)S(1)} %copy-done.1, s32[8]{0:T(128)S(1)} %copy-done.2, bf16[8,8,19008]{2,1,0:T(8,128)(2,1)} %x_hbm.1, bf16[8,8,19008]{2,1,0:T(8,128)(2,1)} %d_hbm.1), custom_call_target="tpu_custom_call" | custom-call | tf_op jit(solution)/shard_map/pallas_call | solution.py:357
  31.6 0.8 %copy.11 = bf16[16,19008]{1,0:T(8,128)(2,1)} copy(bf16[16,19008]{1,0:T(8,128)(2,1)S(1)} %bitcast.3) | data formatting | bytes 1216512
  32.4 0.6 %copy.12 = f32[16,8]{0,1:T(8,128)} copy(f32[16,8]{0,1:T(8,128)S(1)} %bitcast.4) | data formatting | bytes 1024
  33.0 0.5 %copy.13 = f32[16]{0:T(128)} copy(f32[16]{0:T(128)S(1)} %bitcast.5) | data formatting | bytes 128
Async XLA Ops:
  0.6 0.7 %copy-start = (s32[8,8]{1,0:T(8,128)S(1)}, s32[8,8]{1,0:T(8,128)}, u32[]{:S(2)}) copy-start(s32[8,8]{1,0:T(8,128)} %tok_hbm.1) | copy-start | bytes 772
  1.3 0.7 %copy-start.1 = (s32[8]{0:T(128)S(1)}, s32[8]{0:T(128)}, u32[]{:S(2)}) copy-start(s32[8]{0:T(128)} %lens_hbm.1) | copy-start | bytes 100
  2.0 0.7 %copy-start.2 = (s32[8]{0:T(128)S(1)}, s32[8]{0:T(128)}, u32[]{:S(2)}) copy-start(s32[8]{0:T(128)} %own_hbm.1) | copy-start | bytes 100
